TPU v7x, 256 devices: a whole 4x4x8 slice. The times are simulated.
256 devices in a mesh: row: 8 (over x, core), col: 32 (over y, z).
Axes of the slice: x: 4, y: 4, z: 8, core: 2. Of those that a mesh axis runs over, the one named last changes fastest.
Arguments:
- rhs: float32 [8, 32, 8, 4, 128], P('row', 'col'), may hold values from -6 to 6
- diag0: float32 [8, 32, 8, 128], P('row', 'col'), may hold values from 2 to 4
- blocks0: float32 [8, 32, 8, 14, 128, 128], P('row', 'col'), may hold values from -0.1875 to 0.1875
- cols0: int32 [8, 32, 8, 14], P('row', 'col'), may hold values from 0 to 23
- sends0: int32 [8, 32, 4, 4], P('row', 'col'), may hold values from 0 to 7
- pro0: float32 [8, 32, 8, 128, 128], P('row', 'col'), may hold values from -0.5 to 0.5
- agg0: int32 [8, 32, 8], P('row', 'col'), may hold values from 0 to 1
- diag1: float32 [8, 32, 2, 128], P('row', 'col'), may hold values from 2 to 4
- blocks1: float32 [8, 32, 2, 14, 128, 128], P('row', 'col'), may hold values from -0.1875 to 0.1875
- cols1: int32 [8, 32, 2, 14], P('row', 'col'), may hold values from 0 to 9
- sends1: int32 [8, 32, 4, 2], P('row', 'col'), may hold values from 0 to 1
- pro1: float32 [8, 32, 2, 128, 128], P('row', 'col'), may hold values from -0.25 to 0.25
- agg1: int32 [8, 32, 2], P('row', 'col'), may hold values from 0 to 63
- cinv: float32 [8192, 8192], P(('row', 'col')), may hold values from -0.0625 to 0.0625
Outputs:
- solution: float32 [8, 32, 8, 4, 128], P('row', 'col')
Inputs may be any that keep to these rules, and one draw needn't show every extreme that they name: `sends0`: indices of the sender's own fine blocks. `sends1`: indices of the sender's own level-one blocks. `cols0`: indices into the extended fine vector of 24 blocks. `cols1`: indices into the extended level-one vector of 10 blocks. `agg0`: a level-one block of the same partition. `agg1`: a coarsest block, on any partition.
All inputs are finite; a program needn't handle non-finite values.
Results may differ from a plain program's by a relative error of at most 0.0001.
Values sent between devices are 32-bit elements; how exact they have to be, the bound alone decides.
A program may use at most 64 MiB of HBM per device.

v0:
```python
import functools
import jax
import jax.numpy as jnp
from jax import lax
from jax.sharding import Mesh
from jax.sharding import PartitionSpec as P

NU = 2
ROW_COL = ("row_0", "row_1", "col_0", "col_1")
ROW = ("row_0", "row_1")
COL = ("col_0", "col_1")
HIGH = lax.Precision.HIGHEST
OMEGA = 0.3


def extended_2(value, sides, width):
    edges = {}
    for axis, dim in sides:
        size, length = (lax.axis_size(axis), value.shape[dim])
        up = [(i, (i + 1) % size) for i in range(size - 1)]
        last = lax.slice_in_dim(value, length - width, length, axis=dim)
        leading = lax.slice_in_dim(value, 0, width, axis=dim)
        edges[dim] = (
            lax.ppermute(last, axis, up),
            lax.ppermute(leading, axis, [(b, a) for a, b in up]),
        )
    done = []
    for _, dim in sides:
        low, high = edges[dim]
        around = [(width, width) if d in done else (0, 0) for d in range(value.ndim)]
        value = jnp.concatenate([jnp.pad(low, around), value, jnp.pad(high, around)], axis=dim)
        done.append(dim)
    return value


def by_axis(value, axes):
    return functools.reduce(lax.psum, axes, value)


def gather_ghosts(vector, sends):
    packed = vector[sends]
    padded = extended_2(packed[None, None], ((ROW, 0), (COL, 1)), 1)
    return jnp.concatenate(
        [vector, padded[0, 1, 0], padded[2, 1, 1], padded[1, 0, 2], padded[1, 2, 3]], axis=0
    )


def apply_op(vector, diag, blocks, cols, sends):
    extended = gather_ghosts(vector, sends)
    nearby = extended[cols]
    coupled = jnp.einsum("bkij,bkrj->bri", blocks, nearby, precision=HIGH)
    return diag[:, None, :] * vector + coupled


def smooth(vector, right_side, diag, blocks, cols, sends, count):
    for sweep in range(count):
        vector = (
            vector
            + OMEGA * (right_side - apply_op(vector, diag, blocks, cols, sends)) / diag[:, None, :]
        )
    return vector


def on_device(
    rhs, diag0, blocks0, cols0, sends0, pro0, agg0, diag1, blocks1, cols1, sends1, pro1, agg1, cinv
):
    fine_rhs = rhs[0, 0]
    fine_diag = diag0[0, 0]
    fine_blocks = blocks0[0, 0]
    fine_cols = cols0[0, 0]
    fine_sends = sends0[0, 0]
    fine_pro = pro0[0, 0]
    level_diag = diag1[0, 0]
    level_blocks = blocks1[0, 0]
    level_cols = cols1[0, 0]
    level_sends = sends1[0, 0]
    level_pro = pro1[0, 0]
    level_count = level_diag.shape[0]
    block_size = level_diag.shape[1]
    loads = fine_rhs.shape[1]
    coarse_total = cinv.shape[1]
    coarse_count = coarse_total // block_size
    fine_x = OMEGA * fine_rhs / fine_diag[:, None, :]
    fine_x = smooth(fine_x, fine_rhs, fine_diag, fine_blocks, fine_cols, fine_sends, NU - 1)
    fine_res = fine_rhs - apply_op(fine_x, fine_diag, fine_blocks, fine_cols, fine_sends)
    onehot0 = (agg0[0, 0][:, None] == jnp.arange(level_count)).astype(jnp.float32)
    restricted = jnp.einsum("bij,bri->brj", fine_pro, fine_res, precision=HIGH)
    level_rhs = jnp.einsum("bc,brj->crj", onehot0, restricted, precision=HIGH)
    level_x = OMEGA * level_rhs / level_diag[:, None, :]
    level_x = smooth(level_x, level_rhs, level_diag, level_blocks, level_cols, level_sends, NU - 1)
    level_res = level_rhs - apply_op(level_x, level_diag, level_blocks, level_cols, level_sends)
    onehot1 = (agg1[0, 0][:, None] == jnp.arange(coarse_count)).astype(jnp.float32)
    contrib = jnp.einsum("bij,bri->brj", level_pro, level_res, precision=HIGH)
    term = jnp.einsum("bc,brj->rcj", onehot1, contrib, precision=HIGH).reshape(loads, coarse_total)
    coarse_rhs = by_axis(term, ROW_COL)
    own_rows = jnp.einsum("ij,rj->ri", cinv, coarse_rhs, precision=HIGH)
    coarse_x = lax.all_gather(own_rows, ROW_COL, axis=1, tiled=True)
    coarse_blocks = coarse_x.reshape(loads, coarse_count, block_size)
    picked = jnp.einsum("bc,rcj->brj", onehot1, coarse_blocks, precision=HIGH)
    level_x = level_x + jnp.einsum("bij,brj->bri", level_pro, picked, precision=HIGH)
    level_x = smooth(level_x, level_rhs, level_diag, level_blocks, level_cols, level_sends, NU)
    lifted = jnp.einsum("bc,crj->brj", onehot0, level_x, precision=HIGH)
    fine_x = fine_x + jnp.einsum("bij,brj->bri", fine_pro, lifted, precision=HIGH)
    fine_x = smooth(fine_x, fine_rhs, fine_diag, fine_blocks, fine_cols, fine_sends, NU)
    return fine_x[None, None]


def solution(mesh):
    finer = Mesh(mesh.devices.reshape(4, 2, 4, 8), ("row_0", "row_1", "col_0", "col_1"))
    in_specs = (
        P(ROW, COL, None, None, None),
        P(ROW, COL, None, None),
        P(ROW, COL, None, None, None, None),
        P(ROW, COL, None, None),
        P(ROW, COL, None, None),
        P(ROW, COL, None, None, None),
        P(ROW, COL, None),
        P(ROW, COL, None, None),
        P(ROW, COL, None, None, None, None),
        P(ROW, COL, None, None),
        P(ROW, COL, None, None),
        P(ROW, COL, None, None, None),
        P(ROW, COL, None),
        P(ROW_COL, None),
    )
    out_specs = P(ROW, COL, None, None, None)
    return jax.shard_map(
        on_device, mesh=finer, in_specs=in_specs, out_specs=out_specs, check_vma=False
    )
```

profile of v0, /device:TPU:8, one launch (start us, length us, event | category | flops | bytes accessed | tf_op | source)
XLA Modules:
  0.0 488.9 jit_solution(9224719478229903555)
XLA Ops:
  10.3 7.6 %collective-permute-start.3 = (f32[1,1,4,4,4,128]{5,4,3,2,1,0:T(4,128)S(1)}, f32[1,1,4,4,4,128]{5,4,3,2,1,0:T(4,128)S(1)}, u32[]{:S(2)}, u32[]{:S(2)}) collective-permute-start(f32[1,1,4,4,4,128]{5,4,3,2,1,0:T(4,128)S(1)} %bitcast.456), channel_id=1, source_target_pairs={{1,0},{2,1},{3,2},{4,3},{5,4},{6,5},{7,6},{8,7},{9,8},{10,9},{11,1... | collective-permute-start | bytes 98312 | tf_op jit(solution)/shard_map/ppermute | solution.py:25
  17.9 1.9 collective-permute-start.2
  19.8 1.3 collective-permute-start.1
  21.1 3.0 collective-permute-start
  26.6 8.3 %constant_dynamic-update-slice_fusion.9 = (f32[24,4,128]{2,1,0:T(4,128)S(1)}, f32[8,4,128]{2,1,0:T(4,128)S(1)}) fusion(f32[8,14,4,128]{3,2,1,0:T(4,128)S(1)} %bitcast.438, f32[1,1,8,14,128,128]{5,4,3,2,1,0:T(8,128)} %param.16, f32[8,128]{1,0:T(8,128)} %bitcast.448, f32[1,1,8,4,128]{4,3,2,1,0:T(4,128)} %param.14), kind=kOutput, calls=%fused_computation.98 | convolution fusion | flops 88113152 | bytes 7622656 | tf_op jit(solution)/shard_map/bkij,bkrj->bri/dot_general | solution.py:51
  35.5 3.0 collective-permute-start.4
  39.2 6.0 %collective-permute-start.7 = (f32[1,1,4,4,4,128]{5,4,3,2,1,0:T(4,128)S(1)}, f32[1,1,4,4,4,128]{5,4,3,2,1,0:T(4,128)S(1)}, u32[]{:S(2)}, u32[]{:S(2)}) collective-permute-start(f32[1,1,4,4,4,128]{5,4,3,2,1,0:T(4,128)S(1)} %bitcast.461), channel_id=1, source_target_pairs={{1,0},{2,1},{3,2},{4,3},{5,4},{6,5},{7,6},{8,7},{9,8},{10,9},{11,1... | collective-permute-start | bytes 98312 | tf_op jit(solution)/shard_map/ppermute | solution.py:25
  45.2 1.9 collective-permute-start.6
  47.1 1.3 collective-permute-start.5
  49.2 2.0 collective-permute-done.5
  51.2 1.9 collective-permute-done.6
  53.2 1.4 gather_fusion.3
  54.6 9.2 %fusion.64 = f32[8,4,128]{2,1,0:T(4,128)S(1)} fusion(f32[8,14,4,128]{3,2,1,0:T(4,128)} %bitcast.440, f32[1,1,8,14,128,128]{5,4,3,2,1,0:T(8,128)} %param.16, f32[1,1,8,4,128]{4,3,2,1,0:T(4,128)S(1)} %copy-done.4, f32[8,4,128]{2,1,0:T(4,128)} %copy-done.5, f32[8,128]{1,0:T(8,128)} %bitcast.449), kind=kOutput, calls=%fused_computation.50 | convolution fusion | flops 88092672 | bytes 7622656 | tf_op jit(solution)/shard_map/bkij,bkrj->bri/dot_general | solution.py:51
  65.7 1.3 multiply_divide_fusion
  67.0 2.0 gather_fusion.4
  69.7 2.6 collective-permute-start.8
  73.6 5.7 %collective-permute-start.11 = (f32[1,1,4,2,4,128]{5,4,3,2,1,0:T(4,128)S(1)}, f32[1,1,4,2,4,128]{5,4,3,2,1,0:T(4,128)S(1)}, u32[]{:S(2)}, u32[]{:S(2)}) collective-permute-start(f32[1,1,4,2,4,128]{5,4,3,2,1,0:T(4,128)S(1)} %copy.98), channel_id=1, source_target_pairs={{1,0},{2,1},{3,2},{4,3},{5,4},{6,5},{7,6},{8,7},{9,8},{10,9},{11,1... | collective-permute-start | bytes 49160 | tf_op jit(solution)/shard_map/ppermute | solution.py:25
  79.3 1.9 collective-permute-start.10
  81.2 1.3 collective-permute-start.9
  84.9 2.1 collective-permute-done.10
  88.2 2.1 gather_fusion.5
  90.3 3.1 constant_dynamic-update-slice_fusion.19
  93.4 2.0 gather_fusion.6
  96.1 1.9 collective-permute-start.12
  98.0 5.7 %collective-permute-start.15 = (f32[1,1,4,2,4,128]{5,4,3,2,1,0:T(4,128)S(1)}, f32[1,1,4,2,4,128]{5,4,3,2,1,0:T(4,128)S(1)}, u32[]{:S(2)}, u32[]{:S(2)}) collective-permute-start(f32[1,1,4,2,4,128]{5,4,3,2,1,0:T(4,128)S(1)} %copy.104), channel_id=1, source_target_pairs={{1,0},{2,1},{3,2},{4,3},{5,4},{6,5},{7,6},{8,7},{9,8},{10,9},{11,1... | collective-permute-start | bytes 49160 | tf_op jit(solution)/shard_map/ppermute | solution.py:25
  103.7 1.9 collective-permute-start.14
  105.7 1.5 collective-permute-start.13
  109.3 2.1 collective-permute-done.14
  112.7 2.1 gather_fusion.7
  114.7 2.4 fusion.127
  119.2 44.8 %all-reduce.5.cloned.1.call-done = f32[4,8192]{1,0:T(4,128)} async-done(((f32[4,8192]{1,0:T(4,128)}), f32[4,8192]{1,0:T(4,128)}) %all-reduce.5.cloned.1.call-update) | async-done | bytes 131088 | tf_op jit(solution)/shard_map/psum | solution.py:37
  164.1 31.7 %all-reduce.7.cloned.1.call-done = f32[4,8192]{1,0:T(4,128)} async-done(((f32[4,8192]{1,0:T(4,128)}), f32[4,8192]{1,0:T(4,128)}) %all-reduce.7.cloned.1.call-update) | async-done | bytes 131088 | tf_op jit(solution)/shard_map/psum | solution.py:37
  195.9 49.0 %all-reduce.9.cloned.1.call-done = f32[4,8192]{1,0:T(4,128)} async-done(((f32[4,8192]{1,0:T(4,128)}), f32[4,8192]{1,0:T(4,128)}) %all-reduce.9.cloned.1.call-update) | async-done | bytes 131088 | tf_op jit(solution)/shard_map/psum | solution.py:37
  244.8 76.3 %all-reduce.11.cloned.1.call-done = f32[4,8192]{1,0:T(4,128)} async-done(((f32[4,8192]{1,0:T(4,128)}), f32[4,8192]{1,0:T(4,128)}) %all-reduce.11.cloned.1.call-update) | async-done | bytes 131088 | tf_op jit(solution)/shard_map/psum | solution.py:37
  321.2 1.8 convolution_bitcast_fusion.1
  323.0 70.0 %all-gather = f32[256,32,4]{1,2,0:T(4,128)S(1)} all-gather(f32[1,32,4]{1,2,0:T(4,128)S(1)} %convolution_bitcast_fusion.1), channel_id=1, replica_groups=mesh['row_0'=4,'row_1'=2,'col_0'=4,'col_1'=8] {'row_0','row_1','col_0','..., dimensions={0}, use_global_device_ids=true | all-gather | bytes 131584 | tf_op jit(solution)/shard_map/all_gather | solution.py:97
  395.9 1.3 collective-permute-start.16
  397.2 4.6 collective-permute-start.19
  401.8 1.9 collective-permute-start.18
  403.7 1.3 collective-permute-start.17
  405.0 1.8 collective-permute-done.17
  406.8 2.7 collective-permute-done.18
  410.2 2.3 constant_dynamic-update-slice_fusion.29
  413.3 1.3 collective-permute-start.20
  414.6 4.9 %collective-permute-start.23 = (f32[1,1,4,2,4,128]{5,4,3,2,1,0:T(4,128)S(1)}, f32[1,1,4,2,4,128]{5,4,3,2,1,0:T(4,128)S(1)}, u32[]{:S(2)}, u32[]{:S(2)}) collective-permute-start(f32[1,1,4,2,4,128]{5,4,3,2,1,0:T(4,128)S(1)} %copy.119), channel_id=1, source_target_pairs={{1,0},{2,1},{3,2},{4,3},{5,4},{6,5},{7,6},{8,7},{9,8},{10,9},{11,1... | collective-permute-start | bytes 49160 | tf_op jit(solution)/shard_map/ppermute | solution.py:25
  419.5 1.9 collective-permute-start.22
  421.4 1.3 collective-permute-start.21
  422.8 1.8 collective-permute-done.21
  424.5 2.7 collective-permute-done.22
  428.0 2.3 fusion.106
  431.2 1.6 constant_dynamic-update-slice_fusion.34
  433.4 1.3 collective-permute-start.24
  434.7 5.7 %collective-permute-start.27 = (f32[1,1,4,4,4,128]{5,4,3,2,1,0:T(4,128)S(1)}, f32[1,1,4,4,4,128]{5,4,3,2,1,0:T(4,128)S(1)}, u32[]{:S(2)}, u32[]{:S(2)}) collective-permute-start(f32[1,1,4,4,4,128]{5,4,3,2,1,0:T(4,128)S(1)} %bitcast.469), channel_id=1, source_target_pairs={{1,0},{2,1},{3,2},{4,3},{5,4},{6,5},{7,6},{8,7},{9,8},{10,9},{11,1... | collective-permute-start | bytes 98312 | tf_op jit(solution)/shard_map/ppermute | solution.py:25
  440.5 1.9 collective-permute-start.26
  442.4 1.3 collective-permute-start.25
  443.7 1.8 collective-permute-done.25
  445.5 2.9 collective-permute-done.26
  449.2 8.2 %constant_dynamic-update-slice_fusion.39 = (f32[24,4,128]{2,1,0:T(4,128)S(1)}, f32[8,4,128]{2,1,0:T(4,128)S(1)}) fusion(f32[8,4,128]{2,1,0:T(4,128)S(1)} %get-tuple-element.18, f32[8,14,4,128]{3,2,1,0:T(4,128)S(1)} %bitcast.437, f32[1,1,8,14,128,128]{5,4,3,2,1,0:T(8,128)} %param.16, f32[8,128]{1,0:T(8,128)S(1)} %bitcast.450, ...), kind=kOutput, calls=%fused_computation.128 | convolution fusion | flops 88104960 | bytes 7639040 | tf_op jit(solution)/shard_map/bkij,bkrj->bri/dot_general | solution.py:51
  459.3 5.6 %collective-permute-start.31 = (f32[1,1,4,4,4,128]{5,4,3,2,1,0:T(4,128)S(1)}, f32[1,1,4,4,4,128]{5,4,3,2,1,0:T(4,128)S(1)}, u32[]{:S(2)}, u32[]{:S(2)}) collective-permute-start(f32[1,1,4,4,4,128]{5,4,3,2,1,0:T(4,128)S(1)} %bitcast.465), channel_id=1, source_target_pairs={{1,0},{2,1},{3,2},{4,3},{5,4},{6,5},{7,6},{8,7},{9,8},{10,9},{11,1... | collective-permute-start | bytes 98312 | tf_op jit(solution)/shard_map/ppermute | solution.py:25
  464.9 1.9 collective-permute-start.30
  466.8 1.5 collective-permute-start.29
  468.3 1.6 collective-permute-done.29
  469.9 2.9 collective-permute-done.30
  473.5 8.8 %fusion.43 = f32[1,1,8,4,128]{4,3,2,1,0:T(4,128)} fusion(f32[8,4,128]{2,1,0:T(4,128)S(1)} %get-tuple-element.20, f32[8,14,4,128]{3,2,1,0:T(4,128)S(1)} %bitcast.439, f32[1,1,8,14,128,128]{5,4,3,2,1,0:T(8,128)} %param.16, f32[1,1,8,4,128]{4,3,2,1,0:T(4,128)S(1)} %copy-done.4, f32[8,128]{1,0:T(8,128)S(1)} %bitcast.451), kind=kOutput, calls=%fused_computation.43 | convolution fusion | flops 88104960 | bytes 7622656 | tf_op jit(solution)/shard_map/bkij,bkrj->bri/dot_general | solution.py:51
  (129 shorter events, 31.8 us)
Async XLA Ops:
  6.5 83.8 %copy-start = (f32[1,1,2,14,128,128]{5,4,3,2,1,0:T(8,128)S(1)}, f32[1,1,2,14,128,128]{5,4,3,2,1,0:T(8,128)}, u32[]{:S(2)}) copy-start(f32[1,1,2,14,128,128]{5,4,3,2,1,0:T(8,128)} %param.22) | copy-start | bytes 5505028
  6.5 48.1 %copy-start.4 = (f32[1,1,8,4,128]{4,3,2,1,0:T(4,128)S(1)}, f32[1,1,8,4,128]{4,3,2,1,0:T(4,128)}, u32[]{:S(2)}) copy-start(f32[1,1,8,4,128]{4,3,2,1,0:T(4,128)} %param.14) | copy-start | bytes 49156
  6.5 32.0 %copy-start.12 = (s32[1,1,2,14]{3,2,1,0:T(2,128)S(1)}, s32[1,1,2,14]{3,2,1,0:T(2,128)}, u32[]{:S(2)}) copy-start(s32[1,1,2,14]{3,2,1,0:T(2,128)} %param.23) | copy-start | bytes 340
  6.5 157.5 %all-reduce.5.cloned.1.call-start = ((), (), s32[]{:S(2)}) async-start(), calls=%async_computation | async-start | bytes 262144 | tf_op jit(solution)/shard_map/psum | solution.py:37
  8.9 44.2 %copy-start.10 = (s32[1024]{0:T(1024)}, s32[1024]{0:T(1024)S(1)}, u32[]{:S(2)}) copy-start(s32[1024]{0:T(1024)S(1)} %get-tuple-element.22) | copy-start | bytes 12292
  10.3 15.6 %collective-permute-start.3 = (f32[1,1,4,4,4,128]{5,4,3,2,1,0:T(4,128)S(1)}, f32[1,1,4,4,4,128]{5,4,3,2,1,0:T(4,128)S(1)}, u32[]{:S(2)}, u32[]{:S(2)}) collective-permute-start(f32[1,1,4,4,4,128]{5,4,3,2,1,0:T(4,128)S(1)} %bitcast.456), channel_id=1, source_target_pairs={{1,0},{2,1},{3,2},{4,3},{5,4},{6,5},{7,6},{8,7},{9,8},{10,9},{11,1... | collective-permute-start | bytes 98312 | tf_op jit(solution)/shard_map/ppermute | solution.py:25
  17.9 7.9 %collective-permute-start.2 = (f32[1,1,4,4,4,128]{5,4,3,2,1,0:T(4,128)S(1)}, f32[1,1,4,4,4,128]{5,4,3,2,1,0:T(4,128)S(1)}, u32[]{:S(2)}, u32[]{:S(2)}) collective-permute-start(f32[1,1,4,4,4,128]{5,4,3,2,1,0:T(4,128)S(1)} %bitcast.457), channel_id=1, source_target_pairs={{0,1},{1,2},{2,3},{3,4},{4,5},{5,6},{6,7},{7,8},{8,9},{9,10},{10,1... | collective-permute-start | bytes 98312 | tf_op jit(solution)/shard_map/ppermute | solution.py:24
  19.8 5.2 %collective-permute-start.1 = (f32[1,1,4,4,4,128]{5,4,3,2,1,0:T(4,128)S(1)}, f32[1,1,4,4,4,128]{5,4,3,2,1,0:T(4,128)S(1)}, u32[]{:S(2)}, u32[]{:S(2)}) collective-permute-start(f32[1,1,4,4,4,128]{5,4,3,2,1,0:T(4,128)S(1)} %bitcast.458), channel_id=1, source_target_pairs={{32,0},{64,32},{96,64},{128,96},{160,128},{192,160},{224,192},{33,... | collective-permute-start | bytes 98312 | tf_op jit(solution)/shard_map/ppermute | solution.py:25
  21.1 3.9 collective-permute-start
  25.0 28.2 %copy-start.8 = (s32[1024]{0:T(1024)}, s32[1024]{0:T(1024)S(1)}, u32[]{:S(2)}) copy-start(s32[1024]{0:T(1024)S(1)} %pad_clamp_fusion.2) | copy-start | bytes 12292
  26.6 37.2 %copy-start.1 = (f32[1,1,8,128,128]{4,3,2,1,0:T(8,128)S(1)}, f32[1,1,8,128,128]{4,3,2,1,0:T(8,128)}, u32[]{:S(2)}) copy-start(f32[1,1,8,128,128]{4,3,2,1,0:T(8,128)} %param.19) | copy-start | bytes 1572868
  34.9 18.3 %copy-start.5 = (f32[8,4,128]{2,1,0:T(4,128)}, f32[8,4,128]{2,1,0:T(4,128)S(1)}, u32[]{:S(2)}) copy-start(f32[8,4,128]{2,1,0:T(4,128)S(1)} %get-tuple-element.10) | copy-start | bytes 49156
  34.9 286.3 %copy-start.2 = (f32[32,8192]{1,0:T(8,128)S(1)}, f32[32,8192]{1,0:T(8,128)}, u32[]{:S(2)}) copy-start(f32[32,8192]{1,0:T(8,128)} %param.27) | copy-start | bytes 3145732
  35.5 12.9 %collective-permute-start.4 = (f32[1,1,4,4,4,128]{5,4,3,2,1,0:T(4,128)S(1)}, f32[1,1,4,4,4,128]{5,4,3,2,1,0:T(4,128)}, u32[]{:S(2)}, u32[]{:S(2)}) collective-permute-start(f32[1,1,4,4,4,128]{5,4,3,2,1,0:T(4,128)S(1)} %bitcast.460), channel_id=1, source_target_pairs={{0,32},{32,64},{64,96},{96,128},{128,160},{160,192},{192,224},{1,3... | collective-permute-start | bytes 98312 | tf_op jit(solution)/shard_map/ppermute | solution.py:24
  39.2 14.0 %collective-permute-start.7 = (f32[1,1,4,4,4,128]{5,4,3,2,1,0:T(4,128)S(1)}, f32[1,1,4,4,4,128]{5,4,3,2,1,0:T(4,128)S(1)}, u32[]{:S(2)}, u32[]{:S(2)}) collective-permute-start(f32[1,1,4,4,4,128]{5,4,3,2,1,0:T(4,128)S(1)} %bitcast.461), channel_id=1, source_target_pairs={{1,0},{2,1},{3,2},{4,3},{5,4},{6,5},{7,6},{8,7},{9,8},{10,9},{11,1... | collective-permute-start | bytes 98312 | tf_op jit(solution)/shard_map/ppermute | solution.py:25
  45.2 7.9 %collective-permute-start.6 = (f32[1,1,4,4,4,128]{5,4,3,2,1,0:T(4,128)S(1)}, f32[1,1,4,4,4,128]{5,4,3,2,1,0:T(4,128)S(1)}, u32[]{:S(2)}, u32[]{:S(2)}) collective-permute-start(f32[1,1,4,4,4,128]{5,4,3,2,1,0:T(4,128)S(1)} %bitcast.462), channel_id=1, source_target_pairs={{0,1},{1,2},{2,3},{3,4},{4,5},{5,6},{6,7},{7,8},{8,9},{9,10},{10,1... | collective-permute-start | bytes 98312 | tf_op jit(solution)/shard_map/ppermute | solution.py:24
  47.1 4.1 collective-permute-start.5
  54.6 62.6 %copy-start.3 = (f32[1,1,2,128,128]{4,3,2,1,0:T(8,128)S(1)}, f32[1,1,2,128,128]{4,3,2,1,0:T(8,128)}, u32[]{:S(2)}) copy-start(f32[1,1,2,128,128]{4,3,2,1,0:T(8,128)} %param.25) | copy-start | bytes 393220
  65.1 0.6 copy-start.6
  69.7 12.9 %collective-permute-start.8 = (f32[1,1,4,2,4,128]{5,4,3,2,1,0:T(4,128)S(1)}, f32[1,1,4,2,4,128]{5,4,3,2,1,0:T(4,128)S(1)}, u32[]{:S(2)}, u32[]{:S(2)}) collective-permute-start(f32[1,1,4,2,4,128]{5,4,3,2,1,0:T(4,128)S(1)} %copy.98), channel_id=1, source_target_pairs={{0,32},{32,64},{64,96},{96,128},{128,160},{160,192},{192,224},{1,3... | collective-permute-start | bytes 49160 | tf_op jit(solution)/shard_map/ppermute | solution.py:24
  73.6 14.1 %collective-permute-start.11 = (f32[1,1,4,2,4,128]{5,4,3,2,1,0:T(4,128)S(1)}, f32[1,1,4,2,4,128]{5,4,3,2,1,0:T(4,128)S(1)}, u32[]{:S(2)}, u32[]{:S(2)}) collective-permute-start(f32[1,1,4,2,4,128]{5,4,3,2,1,0:T(4,128)S(1)} %copy.98), channel_id=1, source_target_pairs={{1,0},{2,1},{3,2},{4,3},{5,4},{6,5},{7,6},{8,7},{9,8},{10,9},{11,1... | collective-permute-start | bytes 49160 | tf_op jit(solution)/shard_map/ppermute | solution.py:25
  79.3 7.7 %collective-permute-start.10 = (f32[1,1,4,2,4,128]{5,4,3,2,1,0:T(4,128)S(1)}, f32[1,1,4,2,4,128]{5,4,3,2,1,0:T(4,128)S(1)}, u32[]{:S(2)}, u32[]{:S(2)}) collective-permute-start(f32[1,1,4,2,4,128]{5,4,3,2,1,0:T(4,128)S(1)} %copy.98), channel_id=1, source_target_pairs={{0,1},{1,2},{2,3},{3,4},{4,5},{5,6},{6,7},{7,8},{8,9},{9,10},{10,1... | collective-permute-start | bytes 49160 | tf_op jit(solution)/shard_map/ppermute | solution.py:24
  81.2 3.1 collective-permute-start.9
  96.1 11.1 %collective-permute-start.12 = (f32[1,1,4,2,4,128]{5,4,3,2,1,0:T(4,128)S(1)}, f32[1,1,4,2,4,128]{5,4,3,2,1,0:T(4,128)S(1)}, u32[]{:S(2)}, u32[]{:S(2)}) collective-permute-start(f32[1,1,4,2,4,128]{5,4,3,2,1,0:T(4,128)S(1)} %copy.104), channel_id=1, source_target_pairs={{0,32},{32,64},{64,96},{96,128},{128,160},{160,192},{192,224},{1,3... | collective-permute-start | bytes 49160 | tf_op jit(solution)/shard_map/ppermute | solution.py:24
  98.0 14.1 %collective-permute-start.15 = (f32[1,1,4,2,4,128]{5,4,3,2,1,0:T(4,128)S(1)}, f32[1,1,4,2,4,128]{5,4,3,2,1,0:T(4,128)S(1)}, u32[]{:S(2)}, u32[]{:S(2)}) collective-permute-start(f32[1,1,4,2,4,128]{5,4,3,2,1,0:T(4,128)S(1)} %copy.104), channel_id=1, source_target_pairs={{1,0},{2,1},{3,2},{4,3},{5,4},{6,5},{7,6},{8,7},{9,8},{10,9},{11,1... | collective-permute-start | bytes 49160 | tf_op jit(solution)/shard_map/ppermute | solution.py:25
  103.7 7.7 %collective-permute-start.14 = (f32[1,1,4,2,4,128]{5,4,3,2,1,0:T(4,128)S(1)}, f32[1,1,4,2,4,128]{5,4,3,2,1,0:T(4,128)S(1)}, u32[]{:S(2)}, u32[]{:S(2)}) collective-permute-start(f32[1,1,4,2,4,128]{5,4,3,2,1,0:T(4,128)S(1)} %copy.104), channel_id=1, source_target_pairs={{0,1},{1,2},{2,3},{3,4},{4,5},{5,6},{6,7},{7,8},{8,9},{9,10},{10,1... | collective-permute-start | bytes 49160 | tf_op jit(solution)/shard_map/ppermute | solution.py:24
  105.7 3.1 collective-permute-start.13
  119.2 76.6 %all-reduce.7.cloned.1.call-start = ((), (), s32[]{:S(2)}) async-start(), calls=%async_computation.1 | async-start | bytes 262144 | tf_op jit(solution)/shard_map/psum | solution.py:37
  164.0 80.8 %all-reduce.9.cloned.1.call-start = ((), (), s32[]{:S(2)}) async-start(), calls=%async_computation.2 | async-start | bytes 262144 | tf_op jit(solution)/shard_map/psum | solution.py:37
  195.8 125.3 %all-reduce.11.cloned.1.call-start = ((), (), s32[]{:S(2)}) async-start(), calls=%async_computation.3 | async-start | bytes 262144 | tf_op jit(solution)/shard_map/psum | solution.py:37
  323.0 109.8 %copy-start.11 = (s32[1024]{0:T(1024)S(1)}, s32[1024]{0:T(1024)}, u32[]{:S(2)}) copy-start(s32[1024]{0:T(1024)} %copy-done.10) | copy-start | bytes 12292
  323.0 125.4 %copy-start.9 = (s32[1024]{0:T(1024)S(1)}, s32[1024]{0:T(1024)}, u32[]{:S(2)}) copy-start(s32[1024]{0:T(1024)} %copy-done.8) | copy-start | bytes 12292
  323.0 126.2 %copy-start.7 = (f32[1,1,8,128]{3,2,1,0:T(8,128)S(1)}, f32[1,1,8,128]{3,2,1,0:T(8,128)}, u32[]{:S(2)}) copy-start(f32[1,1,8,128]{3,2,1,0:T(8,128)} %param.15) | copy-start | bytes 12292
  395.9 9.1 %collective-permute-start.16 = (f32[1,1,4,2,4,128]{5,4,3,2,1,0:T(4,128)S(1)}, f32[1,1,4,2,4,128]{5,4,3,2,1,0:T(4,128)S(1)}, u32[]{:S(2)}, u32[]{:S(2)}) collective-permute-start(f32[1,1,4,2,4,128]{5,4,3,2,1,0:T(4,128)S(1)} %copy.113), channel_id=1, source_target_pairs={{0,32},{32,64},{64,96},{96,128},{128,160},{160,192},{192,224},{1,3... | collective-permute-start | bytes 49160 | tf_op jit(solution)/shard_map/ppermute | solution.py:24
  397.2 12.4 %collective-permute-start.19 = (f32[1,1,4,2,4,128]{5,4,3,2,1,0:T(4,128)S(1)}, f32[1,1,4,2,4,128]{5,4,3,2,1,0:T(4,128)S(1)}, u32[]{:S(2)}, u32[]{:S(2)}) collective-permute-start(f32[1,1,4,2,4,128]{5,4,3,2,1,0:T(4,128)S(1)} %copy.113), channel_id=1, source_target_pairs={{1,0},{2,1},{3,2},{4,3},{5,4},{6,5},{7,6},{8,7},{9,8},{10,9},{11,1... | collective-permute-start | bytes 49160 | tf_op jit(solution)/shard_map/ppermute | solution.py:25
  401.8 7.7 %collective-permute-start.18 = (f32[1,1,4,2,4,128]{5,4,3,2,1,0:T(4,128)S(1)}, f32[1,1,4,2,4,128]{5,4,3,2,1,0:T(4,128)S(1)}, u32[]{:S(2)}, u32[]{:S(2)}) collective-permute-start(f32[1,1,4,2,4,128]{5,4,3,2,1,0:T(4,128)S(1)} %copy.113), channel_id=1, source_target_pairs={{0,1},{1,2},{2,3},{3,4},{4,5},{5,6},{6,7},{7,8},{8,9},{9,10},{10,1... | collective-permute-start | bytes 49160 | tf_op jit(solution)/shard_map/ppermute | solution.py:24
  403.7 3.1 collective-permute-start.17
  413.3 9.5 %collective-permute-start.20 = (f32[1,1,4,2,4,128]{5,4,3,2,1,0:T(4,128)S(1)}, f32[1,1,4,2,4,128]{5,4,3,2,1,0:T(4,128)S(1)}, u32[]{:S(2)}, u32[]{:S(2)}) collective-permute-start(f32[1,1,4,2,4,128]{5,4,3,2,1,0:T(4,128)S(1)} %copy.119), channel_id=1, source_target_pairs={{0,32},{32,64},{64,96},{96,128},{128,160},{160,192},{192,224},{1,3... | collective-permute-start | bytes 49160 | tf_op jit(solution)/shard_map/ppermute | solution.py:24
  414.6 12.7 %collective-permute-start.23 = (f32[1,1,4,2,4,128]{5,4,3,2,1,0:T(4,128)S(1)}, f32[1,1,4,2,4,128]{5,4,3,2,1,0:T(4,128)S(1)}, u32[]{:S(2)}, u32[]{:S(2)}) collective-permute-start(f32[1,1,4,2,4,128]{5,4,3,2,1,0:T(4,128)S(1)} %copy.119), channel_id=1, source_target_pairs={{1,0},{2,1},{3,2},{4,3},{5,4},{6,5},{7,6},{8,7},{9,8},{10,9},{11,1... | collective-permute-start | bytes 49160 | tf_op jit(solution)/shard_map/ppermute | solution.py:25
  419.5 7.7 %collective-permute-start.22 = (f32[1,1,4,2,4,128]{5,4,3,2,1,0:T(4,128)S(1)}, f32[1,1,4,2,4,128]{5,4,3,2,1,0:T(4,128)S(1)}, u32[]{:S(2)}, u32[]{:S(2)}) collective-permute-start(f32[1,1,4,2,4,128]{5,4,3,2,1,0:T(4,128)S(1)} %copy.119), channel_id=1, source_target_pairs={{0,1},{1,2},{2,3},{3,4},{4,5},{5,6},{6,7},{7,8},{8,9},{9,10},{10,1... | collective-permute-start | bytes 49160 | tf_op jit(solution)/shard_map/ppermute | solution.py:24
  421.4 3.1 collective-permute-start.21
  433.4 10.3 %collective-permute-start.24 = (f32[1,1,4,4,4,128]{5,4,3,2,1,0:T(4,128)S(1)}, f32[1,1,4,4,4,128]{5,4,3,2,1,0:T(4,128)S(1)}, u32[]{:S(2)}, u32[]{:S(2)}) collective-permute-start(f32[1,1,4,4,4,128]{5,4,3,2,1,0:T(4,128)S(1)} %bitcast.468), channel_id=1, source_target_pairs={{0,32},{32,64},{64,96},{96,128},{128,160},{160,192},{192,224},{1,3... | collective-permute-start | bytes 98312 | tf_op jit(solution)/shard_map/ppermute | solution.py:24
  434.7 13.7 %collective-permute-start.27 = (f32[1,1,4,4,4,128]{5,4,3,2,1,0:T(4,128)S(1)}, f32[1,1,4,4,4,128]{5,4,3,2,1,0:T(4,128)S(1)}, u32[]{:S(2)}, u32[]{:S(2)}) collective-permute-start(f32[1,1,4,4,4,128]{5,4,3,2,1,0:T(4,128)S(1)} %bitcast.469), channel_id=1, source_target_pairs={{1,0},{2,1},{3,2},{4,3},{5,4},{6,5},{7,6},{8,7},{9,8},{10,9},{11,1... | collective-permute-start | bytes 98312 | tf_op jit(solution)/shard_map/ppermute | solution.py:25
  440.5 7.9 %collective-permute-start.26 = (f32[1,1,4,4,4,128]{5,4,3,2,1,0:T(4,128)S(1)}, f32[1,1,4,4,4,128]{5,4,3,2,1,0:T(4,128)S(1)}, u32[]{:S(2)}, u32[]{:S(2)}) collective-permute-start(f32[1,1,4,4,4,128]{5,4,3,2,1,0:T(4,128)S(1)} %bitcast.470), channel_id=1, source_target_pairs={{0,1},{1,2},{2,3},{3,4},{4,5},{5,6},{6,7},{7,8},{8,9},{9,10},{10,1... | collective-permute-start | bytes 98312 | tf_op jit(solution)/shard_map/ppermute | solution.py:24
  442.4 3.1 collective-permute-start.25
  458.0 10.3 %collective-permute-start.28 = (f32[1,1,4,4,4,128]{5,4,3,2,1,0:T(4,128)S(1)}, f32[1,1,4,4,4,128]{5,4,3,2,1,0:T(4,128)S(1)}, u32[]{:S(2)}, u32[]{:S(2)}) collective-permute-start(f32[1,1,4,4,4,128]{5,4,3,2,1,0:T(4,128)S(1)} %bitcast.464), channel_id=1, source_target_pairs={{0,32},{32,64},{64,96},{96,128},{128,160},{160,192},{192,224},{1,3... | collective-permute-start | bytes 98312 | tf_op jit(solution)/shard_map/ppermute | solution.py:24
  459.3 13.5 %collective-permute-start.31 = (f32[1,1,4,4,4,128]{5,4,3,2,1,0:T(4,128)S(1)}, f32[1,1,4,4,4,128]{5,4,3,2,1,0:T(4,128)S(1)}, u32[]{:S(2)}, u32[]{:S(2)}) collective-permute-start(f32[1,1,4,4,4,128]{5,4,3,2,1,0:T(4,128)S(1)} %bitcast.465), channel_id=1, source_target_pairs={{1,0},{2,1},{3,2},{4,3},{5,4},{6,5},{7,6},{8,7},{9,8},{10,9},{11,1... | collective-permute-start | bytes 98312 | tf_op jit(solution)/shard_map/ppermute | solution.py:25
  464.9 7.9 %collective-permute-start.30 = (f32[1,1,4,4,4,128]{5,4,3,2,1,0:T(4,128)S(1)}, f32[1,1,4,4,4,128]{5,4,3,2,1,0:T(4,128)S(1)}, u32[]{:S(2)}, u32[]{:S(2)}) collective-permute-start(f32[1,1,4,4,4,128]{5,4,3,2,1,0:T(4,128)S(1)} %bitcast.466), channel_id=1, source_target_pairs={{0,1},{1,2},{2,3},{3,4},{4,5},{5,6},{6,7},{7,8},{8,9},{9,10},{10,1... | collective-permute-start | bytes 98312 | tf_op jit(solution)/shard_map/ppermute | solution.py:24
  466.8 3.1 collective-permute-start.29
Sparse Core Ops, SparseCore 0:
  119.3 44.6 all-reduce.4
  166.6 29.1 all-reduce.6
  198.1 46.6 all-reduce.8
  247.0 74.1 all-reduce.10
where the time goes:
time: 491 us; the launch traced here: 489 us
  waiting for transfers between devices  231 us (47%)
  starting transfers between devices  87.9 us (18%)
  blocking collectives  70 us (14%)
  matrix products  53.4 us (11%)
  local copies, waits for them, and re-layouts  26.7 us (5%)
  between operations  13.6 us (3%)
  other arithmetic  6.11 us (1%)
    psum x4, waiting for transfers between devices, by_axis(): return functools.reduce(lax.psum, axes, value)  202 us
    all_gather x1, blocking collectives, on_device(): coarse_x = lax.all_gather(own_rows, ROW_COL, axis=1, tiled=True)  70 us
    ppermute x16, starting transfers between devices, extended_2(): lax.ppermute(leading, axis, [(b, a) for a, b in up])  56.7 us
    dot_general x8, matrix products, apply_op(): coupled = jnp.einsum('bkij,bkrj->bri', blocks, nearby, precision=HIGH)  44.6 us
    ppermute x16, starting transfers between devices, extended_2(): lax.ppermute(last, axis, up)  31.1 us
    ppermute x16, waiting for transfers between devices, extended_2(): lax.ppermute(last, axis, up)  18.3 us
    ppermute x16, waiting for transfers between devices, extended_2(): lax.ppermute(leading, axis, [(b, a) for a, b in up])  11.1 us
  transfers between devices with their start and end apart: 36, of which 19 were waited for; matrix products, arithmetic and copies ran while one was open for 1% of the time, Pallas kernels for 0%

commit v1 on v0

--- a/solution.py
+++ b/solution.py
@@ -11,6 +11,13 @@
 COL = ("col_0", "col_1")
 HIGH = lax.Precision.HIGHEST
 OMEGA = 0.3
+
+
+def exchange_gather(block, axis, d):
+    n_dev = lax.axis_size(axis)
+    blocks = jnp.stack([block for _ in range(n_dev)])
+    blocks = lax.all_to_all(blocks, axis, split_axis=0, concat_axis=0)
+    return jnp.concatenate(blocks, axis=d)
 
 
 def extended_2(value, sides, width):
@@ -94,7 +101,7 @@
     term = jnp.einsum("bc,brj->rcj", onehot1, contrib, precision=HIGH).reshape(loads, coarse_total)
     coarse_rhs = by_axis(term, ROW_COL)
     own_rows = jnp.einsum("ij,rj->ri", cinv, coarse_rhs, precision=HIGH)
-    coarse_x = lax.all_gather(own_rows, ROW_COL, axis=1, tiled=True)
+    coarse_x = exchange_gather(own_rows, ROW_COL, 1)
     coarse_blocks = coarse_x.reshape(loads, coarse_count, block_size)
     picked = jnp.einsum("bc,rcj->brj", onehot1, coarse_blocks, precision=HIGH)
     level_x = level_x + jnp.einsum("bij,brj->bri", level_pro, picked, precision=HIGH)

time: 491 us -> 445 us (0.906)
  blocking collectives: 70 us -> 22.2 us
    all_gather x1 -> x0, blocking collectives: 70 us -> none  [on_device(): coarse_x = lax.all_gather(own_rows, ROW_COL, axis=1, tiled=True)]
    all_to_all x0 -> x1, blocking collectives: none -> 22.2 us  [exchange_gather(): blocks = lax.all_to_all(blocks, axis, split_axis=0, concat_axis=0)]
  transfers between devices with their start and end apart: 36 -> 36, of which waited for: 19 -> 19; matrix products, arithmetic and copies ran while one was open for 1% -> 2% of each run, Pallas kernels for 0% -> 0%
where the time goes in v1:
time: 445 us; the launch traced here: 443 us
  waiting for transfers between devices  230 us (52%)
  starting transfers between devices  88.9 us (20%)
  matrix products  53.4 us (12%)
  local copies, waits for them, and re-layouts  28 us (6%)
  blocking collectives  22.2 us (5%)
  between operations  13.7 us (3%)
  other arithmetic  7 us (2%)
    psum x4, waiting for transfers between devices, by_axis(): return functools.reduce(lax.psum, axes, value)  202 us
    ppermute x16, starting transfers between devices, extended_2(): lax.ppermute(leading, axis, [(b, a) for a, b in up])  54.9 us
    dot_general x8, matrix products, apply_op(): coupled = jnp.einsum('bkij,bkrj->bri', blocks, nearby, precision=HIGH)  44.7 us
    ppermute x16, starting transfers between devices, extended_2(): lax.ppermute(last, axis, up)  33.9 us
    all_to_all x1, blocking collectives, exchange_gather(): blocks = lax.all_to_all(blocks, axis, split_axis=0, concat_axis=0)  22.2 us
    ppermute x16, waiting for transfers between devices, extended_2(): lax.ppermute(last, axis, up)  17.2 us
    ppermute x16, waiting for transfers between devices, extended_2(): lax.ppermute(leading, axis, [(b, a) for a, b in up])  11.1 us
    gather x12, local copies, waits for them, and re-layouts, gather_ghosts(): packed = vector[sends]  9.3 us
  transfers between devices with their start and end apart: 36, of which 19 were waited for; matrix products, arithmetic and copies ran while one was open for 2% of the time, Pallas kernels for 0%

profile of v1, /device:TPU:8, one launch (start us, length us, event | category | flops | bytes accessed | tf_op | source)
XLA Modules:
  0.0 443.4 jit_solution(13891947544888071292)
XLA Ops:
  10.3 7.6 %collective-permute-start.3 = (f32[1,1,4,4,4,128]{5,4,3,2,1,0:T(4,128)S(1)}, f32[1,1,4,4,4,128]{5,4,3,2,1,0:T(4,128)S(1)}, u32[]{:S(2)}, u32[]{:S(2)}) collective-permute-start(f32[1,1,4,4,4,128]{5,4,3,2,1,0:T(4,128)S(1)} %bitcast.447), channel_id=1, source_target_pairs={{1,0},{2,1},{3,2},{4,3},{5,4},{6,5},{7,6},{8,7},{9,8},{10,9},{11,1... | collective-permute-start | bytes 98312 | tf_op jit(solution)/shard_map/ppermute | solution.py:32
  17.9 1.9 collective-permute-start.2
  19.8 1.3 collective-permute-start.1
  21.1 3.0 collective-permute-start
  26.6 8.3 %constant_dynamic-update-slice_fusion.9 = (f32[24,4,128]{2,1,0:T(4,128)S(1)}, f32[8,4,128]{2,1,0:T(4,128)S(1)}) fusion(f32[8,14,4,128]{3,2,1,0:T(4,128)S(1)} %bitcast.430, f32[1,1,8,14,128,128]{5,4,3,2,1,0:T(8,128)} %param.16, f32[8,128]{1,0:T(8,128)} %bitcast.439, f32[1,1,8,4,128]{4,3,2,1,0:T(4,128)} %param.14), kind=kOutput, calls=%fused_computation.94 | convolution fusion | flops 88113152 | bytes 7622656 | tf_op jit(solution)/shard_map/bkij,bkrj->bri/dot_general | solution.py:58
  35.5 3.0 collective-permute-start.4
  39.1 6.0 %collective-permute-start.7 = (f32[1,1,4,4,4,128]{5,4,3,2,1,0:T(4,128)S(1)}, f32[1,1,4,4,4,128]{5,4,3,2,1,0:T(4,128)S(1)}, u32[]{:S(2)}, u32[]{:S(2)}) collective-permute-start(f32[1,1,4,4,4,128]{5,4,3,2,1,0:T(4,128)S(1)} %bitcast.452), channel_id=1, source_target_pairs={{1,0},{2,1},{3,2},{4,3},{5,4},{6,5},{7,6},{8,7},{9,8},{10,9},{11,1... | collective-permute-start | bytes 98312 | tf_op jit(solution)/shard_map/ppermute | solution.py:32
  45.2 1.9 collective-permute-start.6
  47.1 1.3 collective-permute-start.5
  49.1 2.0 collective-permute-done.5
  51.2 1.9 collective-permute-done.6
  53.1 1.4 gather_fusion.3
  54.5 9.2 %fusion.64 = f32[8,4,128]{2,1,0:T(4,128)S(1)} fusion(f32[8,14,4,128]{3,2,1,0:T(4,128)} %bitcast.432, f32[1,1,8,14,128,128]{5,4,3,2,1,0:T(8,128)} %param.16, f32[1,1,8,4,128]{4,3,2,1,0:T(4,128)S(1)} %copy-done.4, f32[8,4,128]{2,1,0:T(4,128)} %copy-done.5, f32[8,128]{1,0:T(8,128)} %bitcast.440), kind=kOutput, calls=%fused_computation.50 | convolution fusion | flops 88092672 | bytes 7622656 | tf_op jit(solution)/shard_map/bkij,bkrj->bri/dot_general | solution.py:58
  67.0 2.0 gather_fusion.4
  69.7 2.6 collective-permute-start.8
  73.5 5.7 %collective-permute-start.11 = (f32[1,1,4,2,4,128]{5,4,3,2,1,0:T(4,128)S(1)}, f32[1,1,4,2,4,128]{5,4,3,2,1,0:T(4,128)S(1)}, u32[]{:S(2)}, u32[]{:S(2)}) collective-permute-start(f32[1,1,4,2,4,128]{5,4,3,2,1,0:T(4,128)S(1)} %copy.97), channel_id=1, source_target_pairs={{1,0},{2,1},{3,2},{4,3},{5,4},{6,5},{7,6},{8,7},{9,8},{10,9},{11,1... | collective-permute-start | bytes 49160 | tf_op jit(solution)/shard_map/ppermute | solution.py:32
  79.3 1.9 collective-permute-start.10
  81.2 1.3 collective-permute-start.9
  84.9 2.1 collective-permute-done.10
  88.2 2.1 gather_fusion.5
  90.2 3.1 constant_dynamic-update-slice_fusion.19
  93.3 2.0 gather_fusion.6
  96.0 1.9 collective-permute-start.12
  97.9 5.7 %collective-permute-start.15 = (f32[1,1,4,2,4,128]{5,4,3,2,1,0:T(4,128)S(1)}, f32[1,1,4,2,4,128]{5,4,3,2,1,0:T(4,128)S(1)}, u32[]{:S(2)}, u32[]{:S(2)}) collective-permute-start(f32[1,1,4,2,4,128]{5,4,3,2,1,0:T(4,128)S(1)} %copy.103), channel_id=1, source_target_pairs={{1,0},{2,1},{3,2},{4,3},{5,4},{6,5},{7,6},{8,7},{9,8},{10,9},{11,1... | collective-permute-start | bytes 49160 | tf_op jit(solution)/shard_map/ppermute | solution.py:32
  103.6 1.9 collective-permute-start.14
  105.6 1.5 collective-permute-start.13
  109.3 2.1 collective-permute-done.14
  112.6 2.1 gather_fusion.7
  114.6 2.4 fusion.127
  119.1 44.8 %all-reduce.5.cloned.1.call-done = f32[4,8192]{1,0:T(4,128)} async-done(((f32[4,8192]{1,0:T(4,128)}), f32[4,8192]{1,0:T(4,128)}) %all-reduce.5.cloned.1.call-update) | async-done | bytes 131088 | tf_op jit(solution)/shard_map/psum | solution.py:44
  164.0 31.7 %all-reduce.7.cloned.1.call-done = f32[4,8192]{1,0:T(4,128)} async-done(((f32[4,8192]{1,0:T(4,128)}), f32[4,8192]{1,0:T(4,128)}) %all-reduce.7.cloned.1.call-update) | async-done | bytes 131088 | tf_op jit(solution)/shard_map/psum | solution.py:44
  195.8 49.0 %all-reduce.9.cloned.1.call-done = f32[4,8192]{1,0:T(4,128)} async-done(((f32[4,8192]{1,0:T(4,128)}), f32[4,8192]{1,0:T(4,128)}) %all-reduce.9.cloned.1.call-update) | async-done | bytes 131088 | tf_op jit(solution)/shard_map/psum | solution.py:44
  244.7 76.3 %all-reduce.11.cloned.1.call-done = f32[4,8192]{1,0:T(4,128)} async-done(((f32[4,8192]{1,0:T(4,128)}), f32[4,8192]{1,0:T(4,128)}) %all-reduce.11.cloned.1.call-update) | async-done | bytes 131088 | tf_op jit(solution)/shard_map/psum | solution.py:44
  321.1 1.8 fusion.168
  323.3 22.2 %all_to_all.5 = f32[256,1,128]{2,1,0:T(1,128)S(1)} all-to-all(f32[256,1,128]{2,1,0:T(1,128)S(1)} %reshape.288), channel_id=1, replica_groups=mesh['row_0'=4,'row_1'=2,'col_0'=4,'col_1'=8] {'row_0','row_1','col_0','..., dimensions={0} | all-to-all | bytes 262144 | tf_op jit(solution)/shard_map/all_to_all | solution.py:19
  350.1 1.9 collective-permute-start.16
  352.0 2.8 collective-permute-start.19
  354.8 3.1 collective-permute-start.18
  357.8 1.3 collective-permute-start.17
  359.2 1.8 collective-permute-done.17
  360.9 1.7 collective-permute-done.18
  363.4 2.3 constant_dynamic-update-slice_fusion.29
  366.4 2.4 collective-permute-start.20
  368.8 5.5 %collective-permute-start.23 = (f32[1,1,4,2,4,128]{5,4,3,2,1,0:T(4,128)S(1)}, f32[1,1,4,2,4,128]{5,4,3,2,1,0:T(4,128)S(1)}, u32[]{:S(2)}, u32[]{:S(2)}) collective-permute-start(f32[1,1,4,2,4,128]{5,4,3,2,1,0:T(4,128)S(1)} %copy.118), channel_id=1, source_target_pairs={{1,0},{2,1},{3,2},{4,3},{5,4},{6,5},{7,6},{8,7},{9,8},{10,9},{11,1... | collective-permute-start | bytes 49160 | tf_op jit(solution)/shard_map/ppermute | solution.py:32
  374.3 1.9 collective-permute-start.22
  376.2 1.3 collective-permute-start.21
  377.5 1.8 collective-permute-done.21
  379.3 2.7 collective-permute-done.22
  382.8 2.3 fusion.106
  385.9 1.6 constant_dynamic-update-slice_fusion.34
  388.3 1.3 collective-permute-start.24
  389.6 5.4 %collective-permute-start.27 = (f32[1,1,4,4,4,128]{5,4,3,2,1,0:T(4,128)S(1)}, f32[1,1,4,4,4,128]{5,4,3,2,1,0:T(4,128)S(1)}, u32[]{:S(2)}, u32[]{:S(2)}) collective-permute-start(f32[1,1,4,4,4,128]{5,4,3,2,1,0:T(4,128)S(1)} %bitcast.460), channel_id=1, source_target_pairs={{1,0},{2,1},{3,2},{4,3},{5,4},{6,5},{7,6},{8,7},{9,8},{10,9},{11,1... | collective-permute-start | bytes 98312 | tf_op jit(solution)/shard_map/ppermute | solution.py:32
  395.0 1.9 collective-permute-start.26
  396.9 1.5 collective-permute-start.25
  398.4 1.6 collective-permute-done.25
  400.0 2.9 collective-permute-done.26
  403.8 8.2 %constant_dynamic-update-slice_fusion.39 = (f32[24,4,128]{2,1,0:T(4,128)S(1)}, f32[8,4,128]{2,1,0:T(4,128)S(1)}) fusion(f32[8,4,128]{2,1,0:T(4,128)S(1)} %get-tuple-element.18, f32[8,14,4,128]{3,2,1,0:T(4,128)S(1)} %bitcast.429, f32[1,1,8,14,128,128]{5,4,3,2,1,0:T(8,128)} %param.16, f32[8,128]{1,0:T(8,128)} %bitcast.441, f32[1,1,8,4,128]{4,3,2,1,0:T(4,128)S(1)} %copy-done.4), kind=kOutput, calls=%fused_computation.124 | convolution fusion | flops 88104960 | bytes 7639040 | tf_op jit(solution)/shard_map/bkij,bkrj->bri/dot_general | solution.py:58
  412.6 1.3 collective-permute-start.28
  413.9 5.4 %collective-permute-start.31 = (f32[1,1,4,4,4,128]{5,4,3,2,1,0:T(4,128)S(1)}, f32[1,1,4,4,4,128]{5,4,3,2,1,0:T(4,128)S(1)}, u32[]{:S(2)}, u32[]{:S(2)}) collective-permute-start(f32[1,1,4,4,4,128]{5,4,3,2,1,0:T(4,128)S(1)} %bitcast.456), channel_id=1, source_target_pairs={{1,0},{2,1},{3,2},{4,3},{5,4},{6,5},{7,6},{8,7},{9,8},{10,9},{11,1... | collective-permute-start | bytes 98312 | tf_op jit(solution)/shard_map/ppermute | solution.py:32
  419.3 1.9 collective-permute-start.30
  421.2 1.3 collective-permute-start.29
  422.5 1.8 collective-permute-done.29
  424.3 2.9 collective-permute-done.30
  428.0 8.8 %fusion.43 = f32[1,1,8,4,128]{4,3,2,1,0:T(4,128)} fusion(f32[8,4,128]{2,1,0:T(4,128)S(1)} %get-tuple-element.20, f32[8,14,4,128]{3,2,1,0:T(4,128)S(1)} %bitcast.431, f32[1,1,8,14,128,128]{5,4,3,2,1,0:T(8,128)} %param.16, f32[1,1,8,4,128]{4,3,2,1,0:T(4,128)S(1)} %copy-done.4, f32[8,128]{1,0:T(8,128)S(1)} %bitcast.442), kind=kOutput, calls=%fused_computation.43 | convolution fusion | flops 88104960 | bytes 7622656 | tf_op jit(solution)/shard_map/bkij,bkrj->bri/dot_general | solution.py:58
  (134 shorter events, 34.0 us)
Async XLA Ops:
  6.5 83.7 %copy-start = (f32[1,1,2,14,128,128]{5,4,3,2,1,0:T(8,128)S(1)}, f32[1,1,2,14,128,128]{5,4,3,2,1,0:T(8,128)}, u32[]{:S(2)}) copy-start(f32[1,1,2,14,128,128]{5,4,3,2,1,0:T(8,128)} %param.22) | copy-start | bytes 5505028
  6.5 48.0 %copy-start.4 = (f32[1,1,8,4,128]{4,3,2,1,0:T(4,128)S(1)}, f32[1,1,8,4,128]{4,3,2,1,0:T(4,128)}, u32[]{:S(2)}) copy-start(f32[1,1,8,4,128]{4,3,2,1,0:T(4,128)} %param.14) | copy-start | bytes 49156
  6.5 32.0 %copy-start.12 = (s32[1,1,2,14]{3,2,1,0:T(2,128)S(1)}, s32[1,1,2,14]{3,2,1,0:T(2,128)}, u32[]{:S(2)}) copy-start(s32[1,1,2,14]{3,2,1,0:T(2,128)} %param.23) | copy-start | bytes 340
  6.5 157.4 %all-reduce.5.cloned.1.call-start = ((), (), s32[]{:S(2)}) async-start(), calls=%async_computation.1 | async-start | bytes 262144 | tf_op jit(solution)/shard_map/psum | solution.py:44
  8.9 44.2 %copy-start.10 = (s32[1024]{0:T(1024)}, s32[1024]{0:T(1024)S(1)}, u32[]{:S(2)}) copy-start(s32[1024]{0:T(1024)S(1)} %get-tuple-element.22) | copy-start | bytes 12292
  10.3 15.6 %collective-permute-start.3 = (f32[1,1,4,4,4,128]{5,4,3,2,1,0:T(4,128)S(1)}, f32[1,1,4,4,4,128]{5,4,3,2,1,0:T(4,128)S(1)}, u32[]{:S(2)}, u32[]{:S(2)}) collective-permute-start(f32[1,1,4,4,4,128]{5,4,3,2,1,0:T(4,128)S(1)} %bitcast.447), channel_id=1, source_target_pairs={{1,0},{2,1},{3,2},{4,3},{5,4},{6,5},{7,6},{8,7},{9,8},{10,9},{11,1... | collective-permute-start | bytes 98312 | tf_op jit(solution)/shard_map/ppermute | solution.py:32
  17.9 7.9 %collective-permute-start.2 = (f32[1,1,4,4,4,128]{5,4,3,2,1,0:T(4,128)S(1)}, f32[1,1,4,4,4,128]{5,4,3,2,1,0:T(4,128)S(1)}, u32[]{:S(2)}, u32[]{:S(2)}) collective-permute-start(f32[1,1,4,4,4,128]{5,4,3,2,1,0:T(4,128)S(1)} %bitcast.448), channel_id=1, source_target_pairs={{0,1},{1,2},{2,3},{3,4},{4,5},{5,6},{6,7},{7,8},{8,9},{9,10},{10,1... | collective-permute-start | bytes 98312 | tf_op jit(solution)/shard_map/ppermute | solution.py:31
  19.8 5.2 %collective-permute-start.1 = (f32[1,1,4,4,4,128]{5,4,3,2,1,0:T(4,128)S(1)}, f32[1,1,4,4,4,128]{5,4,3,2,1,0:T(4,128)S(1)}, u32[]{:S(2)}, u32[]{:S(2)}) collective-permute-start(f32[1,1,4,4,4,128]{5,4,3,2,1,0:T(4,128)S(1)} %bitcast.449), channel_id=1, source_target_pairs={{32,0},{64,32},{96,64},{128,96},{160,128},{192,160},{224,192},{33,... | collective-permute-start | bytes 98312 | tf_op jit(solution)/shard_map/ppermute | solution.py:32
  21.1 3.9 collective-permute-start
  25.0 28.1 %copy-start.8 = (s32[1024]{0:T(1024)}, s32[1024]{0:T(1024)S(1)}, u32[]{:S(2)}) copy-start(s32[1024]{0:T(1024)S(1)} %pad_clamp_fusion.2) | copy-start | bytes 12292
  26.6 37.2 %copy-start.1 = (f32[1,1,8,128,128]{4,3,2,1,0:T(8,128)S(1)}, f32[1,1,8,128,128]{4,3,2,1,0:T(8,128)}, u32[]{:S(2)}) copy-start(f32[1,1,8,128,128]{4,3,2,1,0:T(8,128)} %param.19) | copy-start | bytes 1572868
  34.9 18.2 %copy-start.5 = (f32[8,4,128]{2,1,0:T(4,128)}, f32[8,4,128]{2,1,0:T(4,128)S(1)}, u32[]{:S(2)}) copy-start(f32[8,4,128]{2,1,0:T(4,128)S(1)} %get-tuple-element.10) | copy-start | bytes 49156
  34.9 286.1 %copy-start.2 = (f32[32,8192]{1,0:T(8,128)S(1)}, f32[32,8192]{1,0:T(8,128)}, u32[]{:S(2)}) copy-start(f32[32,8192]{1,0:T(8,128)} %param.27) | copy-start | bytes 3145732
  35.5 12.9 %collective-permute-start.4 = (f32[1,1,4,4,4,128]{5,4,3,2,1,0:T(4,128)S(1)}, f32[1,1,4,4,4,128]{5,4,3,2,1,0:T(4,128)}, u32[]{:S(2)}, u32[]{:S(2)}) collective-permute-start(f32[1,1,4,4,4,128]{5,4,3,2,1,0:T(4,128)S(1)} %bitcast.451), channel_id=1, source_target_pairs={{0,32},{32,64},{64,96},{96,128},{128,160},{160,192},{192,224},{1,3... | collective-permute-start | bytes 98312 | tf_op jit(solution)/shard_map/ppermute | solution.py:31
  39.1 14.0 %collective-permute-start.7 = (f32[1,1,4,4,4,128]{5,4,3,2,1,0:T(4,128)S(1)}, f32[1,1,4,4,4,128]{5,4,3,2,1,0:T(4,128)S(1)}, u32[]{:S(2)}, u32[]{:S(2)}) collective-permute-start(f32[1,1,4,4,4,128]{5,4,3,2,1,0:T(4,128)S(1)} %bitcast.452), channel_id=1, source_target_pairs={{1,0},{2,1},{3,2},{4,3},{5,4},{6,5},{7,6},{8,7},{9,8},{10,9},{11,1... | collective-permute-start | bytes 98312 | tf_op jit(solution)/shard_map/ppermute | solution.py:32
  45.2 7.9 %collective-permute-start.6 = (f32[1,1,4,4,4,128]{5,4,3,2,1,0:T(4,128)S(1)}, f32[1,1,4,4,4,128]{5,4,3,2,1,0:T(4,128)S(1)}, u32[]{:S(2)}, u32[]{:S(2)}) collective-permute-start(f32[1,1,4,4,4,128]{5,4,3,2,1,0:T(4,128)S(1)} %bitcast.453), channel_id=1, source_target_pairs={{0,1},{1,2},{2,3},{3,4},{4,5},{5,6},{6,7},{7,8},{8,9},{9,10},{10,1... | collective-permute-start | bytes 98312 | tf_op jit(solution)/shard_map/ppermute | solution.py:31
  47.1 4.1 collective-permute-start.5
  54.5 62.5 %copy-start.3 = (f32[1,1,2,128,128]{4,3,2,1,0:T(8,128)S(1)}, f32[1,1,2,128,128]{4,3,2,1,0:T(8,128)}, u32[]{:S(2)}) copy-start(f32[1,1,2,128,128]{4,3,2,1,0:T(8,128)} %param.25) | copy-start | bytes 393220
  65.1 0.6 copy-start.6
  69.7 12.8 %collective-permute-start.8 = (f32[1,1,4,2,4,128]{5,4,3,2,1,0:T(4,128)S(1)}, f32[1,1,4,2,4,128]{5,4,3,2,1,0:T(4,128)S(1)}, u32[]{:S(2)}, u32[]{:S(2)}) collective-permute-start(f32[1,1,4,2,4,128]{5,4,3,2,1,0:T(4,128)S(1)} %copy.97), channel_id=1, source_target_pairs={{0,32},{32,64},{64,96},{96,128},{128,160},{160,192},{192,224},{1,3... | collective-permute-start | bytes 49160 | tf_op jit(solution)/shard_map/ppermute | solution.py:31
  73.5 14.1 %collective-permute-start.11 = (f32[1,1,4,2,4,128]{5,4,3,2,1,0:T(4,128)S(1)}, f32[1,1,4,2,4,128]{5,4,3,2,1,0:T(4,128)S(1)}, u32[]{:S(2)}, u32[]{:S(2)}) collective-permute-start(f32[1,1,4,2,4,128]{5,4,3,2,1,0:T(4,128)S(1)} %copy.97), channel_id=1, source_target_pairs={{1,0},{2,1},{3,2},{4,3},{5,4},{6,5},{7,6},{8,7},{9,8},{10,9},{11,1... | collective-permute-start | bytes 49160 | tf_op jit(solution)/shard_map/ppermute | solution.py:32
  79.3 7.7 %collective-permute-start.10 = (f32[1,1,4,2,4,128]{5,4,3,2,1,0:T(4,128)S(1)}, f32[1,1,4,2,4,128]{5,4,3,2,1,0:T(4,128)S(1)}, u32[]{:S(2)}, u32[]{:S(2)}) collective-permute-start(f32[1,1,4,2,4,128]{5,4,3,2,1,0:T(4,128)S(1)} %copy.97), channel_id=1, source_target_pairs={{0,1},{1,2},{2,3},{3,4},{4,5},{5,6},{6,7},{7,8},{8,9},{9,10},{10,1... | collective-permute-start | bytes 49160 | tf_op jit(solution)/shard_map/ppermute | solution.py:31
  81.2 3.1 collective-permute-start.9
  96.0 11.1 %collective-permute-start.12 = (f32[1,1,4,2,4,128]{5,4,3,2,1,0:T(4,128)S(1)}, f32[1,1,4,2,4,128]{5,4,3,2,1,0:T(4,128)S(1)}, u32[]{:S(2)}, u32[]{:S(2)}) collective-permute-start(f32[1,1,4,2,4,128]{5,4,3,2,1,0:T(4,128)S(1)} %copy.103), channel_id=1, source_target_pairs={{0,32},{32,64},{64,96},{96,128},{128,160},{160,192},{192,224},{1,3... | collective-permute-start | bytes 49160 | tf_op jit(solution)/shard_map/ppermute | solution.py:31
  97.9 14.1 %collective-permute-start.15 = (f32[1,1,4,2,4,128]{5,4,3,2,1,0:T(4,128)S(1)}, f32[1,1,4,2,4,128]{5,4,3,2,1,0:T(4,128)S(1)}, u32[]{:S(2)}, u32[]{:S(2)}) collective-permute-start(f32[1,1,4,2,4,128]{5,4,3,2,1,0:T(4,128)S(1)} %copy.103), channel_id=1, source_target_pairs={{1,0},{2,1},{3,2},{4,3},{5,4},{6,5},{7,6},{8,7},{9,8},{10,9},{11,1... | collective-permute-start | bytes 49160 | tf_op jit(solution)/shard_map/ppermute | solution.py:32
  103.6 7.7 %collective-permute-start.14 = (f32[1,1,4,2,4,128]{5,4,3,2,1,0:T(4,128)S(1)}, f32[1,1,4,2,4,128]{5,4,3,2,1,0:T(4,128)S(1)}, u32[]{:S(2)}, u32[]{:S(2)}) collective-permute-start(f32[1,1,4,2,4,128]{5,4,3,2,1,0:T(4,128)S(1)} %copy.103), channel_id=1, source_target_pairs={{0,1},{1,2},{2,3},{3,4},{4,5},{5,6},{6,7},{7,8},{8,9},{9,10},{10,1... | collective-permute-start | bytes 49160 | tf_op jit(solution)/shard_map/ppermute | solution.py:31
  105.6 3.1 collective-permute-start.13
  119.1 76.6 %all-reduce.7.cloned.1.call-start = ((), (), s32[]{:S(2)}) async-start(), calls=%async_computation.2 | async-start | bytes 262144 | tf_op jit(solution)/shard_map/psum | solution.py:44
  163.9 80.8 %all-reduce.9.cloned.1.call-start = ((), (), s32[]{:S(2)}) async-start(), calls=%async_computation.3 | async-start | bytes 262144 | tf_op jit(solution)/shard_map/psum | solution.py:44
  195.7 125.3 %all-reduce.11.cloned.1.call-start = ((), (), s32[]{:S(2)}) async-start(), calls=%async_computation.4 | async-start | bytes 262144 | tf_op jit(solution)/shard_map/psum | solution.py:44
  347.3 64.7 %copy-start.11 = (s32[1024]{0:T(1024)S(1)}, s32[1024]{0:T(1024)}, u32[]{:S(2)}) copy-start(s32[1024]{0:T(1024)} %copy-done.10) | copy-start | bytes 12292
  347.3 79.9 %copy-start.9 = (s32[1024]{0:T(1024)S(1)}, s32[1024]{0:T(1024)}, u32[]{:S(2)}) copy-start(s32[1024]{0:T(1024)} %copy-done.8) | copy-start | bytes 12292
  347.3 80.6 %copy-start.7 = (f32[1,1,8,128]{3,2,1,0:T(8,128)S(1)}, f32[1,1,8,128]{3,2,1,0:T(8,128)}, u32[]{:S(2)}) copy-start(f32[1,1,8,128]{3,2,1,0:T(8,128)} %param.15) | copy-start | bytes 12292
  350.1 9.1 %collective-permute-start.16 = (f32[1,1,4,2,4,128]{5,4,3,2,1,0:T(4,128)S(1)}, f32[1,1,4,2,4,128]{5,4,3,2,1,0:T(4,128)S(1)}, u32[]{:S(2)}, u32[]{:S(2)}) collective-permute-start(f32[1,1,4,2,4,128]{5,4,3,2,1,0:T(4,128)S(1)} %copy.112), channel_id=1, source_target_pairs={{0,32},{32,64},{64,96},{96,128},{128,160},{160,192},{192,224},{1,3... | collective-permute-start | bytes 49160 | tf_op jit(solution)/shard_map/ppermute | solution.py:31
  352.0 10.7 %collective-permute-start.19 = (f32[1,1,4,2,4,128]{5,4,3,2,1,0:T(4,128)S(1)}, f32[1,1,4,2,4,128]{5,4,3,2,1,0:T(4,128)S(1)}, u32[]{:S(2)}, u32[]{:S(2)}) collective-permute-start(f32[1,1,4,2,4,128]{5,4,3,2,1,0:T(4,128)S(1)} %copy.112), channel_id=1, source_target_pairs={{1,0},{2,1},{3,2},{4,3},{5,4},{6,5},{7,6},{8,7},{9,8},{10,9},{11,1... | collective-permute-start | bytes 49160 | tf_op jit(solution)/shard_map/ppermute | solution.py:32
  354.8 7.9 %collective-permute-start.18 = (f32[1,1,4,2,4,128]{5,4,3,2,1,0:T(4,128)S(1)}, f32[1,1,4,2,4,128]{5,4,3,2,1,0:T(4,128)S(1)}, u32[]{:S(2)}, u32[]{:S(2)}) collective-permute-start(f32[1,1,4,2,4,128]{5,4,3,2,1,0:T(4,128)S(1)} %copy.112), channel_id=1, source_target_pairs={{0,1},{1,2},{2,3},{3,4},{4,5},{5,6},{6,7},{7,8},{8,9},{9,10},{10,1... | collective-permute-start | bytes 49160 | tf_op jit(solution)/shard_map/ppermute | solution.py:31
  357.8 3.1 collective-permute-start.17
  366.4 11.1 %collective-permute-start.20 = (f32[1,1,4,2,4,128]{5,4,3,2,1,0:T(4,128)S(1)}, f32[1,1,4,2,4,128]{5,4,3,2,1,0:T(4,128)S(1)}, u32[]{:S(2)}, u32[]{:S(2)}) collective-permute-start(f32[1,1,4,2,4,128]{5,4,3,2,1,0:T(4,128)S(1)} %copy.118), channel_id=1, source_target_pairs={{0,32},{32,64},{64,96},{96,128},{128,160},{160,192},{192,224},{1,3... | collective-permute-start | bytes 49160 | tf_op jit(solution)/shard_map/ppermute | solution.py:31
  368.8 13.2 %collective-permute-start.23 = (f32[1,1,4,2,4,128]{5,4,3,2,1,0:T(4,128)S(1)}, f32[1,1,4,2,4,128]{5,4,3,2,1,0:T(4,128)S(1)}, u32[]{:S(2)}, u32[]{:S(2)}) collective-permute-start(f32[1,1,4,2,4,128]{5,4,3,2,1,0:T(4,128)S(1)} %copy.118), channel_id=1, source_target_pairs={{1,0},{2,1},{3,2},{4,3},{5,4},{6,5},{7,6},{8,7},{9,8},{10,9},{11,1... | collective-permute-start | bytes 49160 | tf_op jit(solution)/shard_map/ppermute | solution.py:32
  374.3 7.7 %collective-permute-start.22 = (f32[1,1,4,2,4,128]{5,4,3,2,1,0:T(4,128)S(1)}, f32[1,1,4,2,4,128]{5,4,3,2,1,0:T(4,128)S(1)}, u32[]{:S(2)}, u32[]{:S(2)}) collective-permute-start(f32[1,1,4,2,4,128]{5,4,3,2,1,0:T(4,128)S(1)} %copy.118), channel_id=1, source_target_pairs={{0,1},{1,2},{2,3},{3,4},{4,5},{5,6},{6,7},{7,8},{8,9},{9,10},{10,1... | collective-permute-start | bytes 49160 | tf_op jit(solution)/shard_map/ppermute | solution.py:31
  376.2 3.1 collective-permute-start.21
  388.3 10.1 %collective-permute-start.24 = (f32[1,1,4,4,4,128]{5,4,3,2,1,0:T(4,128)S(1)}, f32[1,1,4,4,4,128]{5,4,3,2,1,0:T(4,128)S(1)}, u32[]{:S(2)}, u32[]{:S(2)}) collective-permute-start(f32[1,1,4,4,4,128]{5,4,3,2,1,0:T(4,128)S(1)} %bitcast.459), channel_id=1, source_target_pairs={{0,32},{32,64},{64,96},{96,128},{128,160},{160,192},{192,224},{1,3... | collective-permute-start | bytes 98312 | tf_op jit(solution)/shard_map/ppermute | solution.py:31
  389.6 13.3 %collective-permute-start.27 = (f32[1,1,4,4,4,128]{5,4,3,2,1,0:T(4,128)S(1)}, f32[1,1,4,4,4,128]{5,4,3,2,1,0:T(4,128)S(1)}, u32[]{:S(2)}, u32[]{:S(2)}) collective-permute-start(f32[1,1,4,4,4,128]{5,4,3,2,1,0:T(4,128)S(1)} %bitcast.460), channel_id=1, source_target_pairs={{1,0},{2,1},{3,2},{4,3},{5,4},{6,5},{7,6},{8,7},{9,8},{10,9},{11,1... | collective-permute-start | bytes 98312 | tf_op jit(solution)/shard_map/ppermute | solution.py:32
  395.0 7.9 %collective-permute-start.26 = (f32[1,1,4,4,4,128]{5,4,3,2,1,0:T(4,128)S(1)}, f32[1,1,4,4,4,128]{5,4,3,2,1,0:T(4,128)S(1)}, u32[]{:S(2)}, u32[]{:S(2)}) collective-permute-start(f32[1,1,4,4,4,128]{5,4,3,2,1,0:T(4,128)S(1)} %bitcast.461), channel_id=1, source_target_pairs={{0,1},{1,2},{2,3},{3,4},{4,5},{5,6},{6,7},{7,8},{8,9},{9,10},{10,1... | collective-permute-start | bytes 98312 | tf_op jit(solution)/shard_map/ppermute | solution.py:31
  396.9 3.1 collective-permute-start.25
  412.6 9.9 %collective-permute-start.28 = (f32[1,1,4,4,4,128]{5,4,3,2,1,0:T(4,128)S(1)}, f32[1,1,4,4,4,128]{5,4,3,2,1,0:T(4,128)S(1)}, u32[]{:S(2)}, u32[]{:S(2)}) collective-permute-start(f32[1,1,4,4,4,128]{5,4,3,2,1,0:T(4,128)S(1)} %bitcast.455), channel_id=1, source_target_pairs={{0,32},{32,64},{64,96},{96,128},{128,160},{160,192},{192,224},{1,3... | collective-permute-start | bytes 98312 | tf_op jit(solution)/shard_map/ppermute | solution.py:31
  413.9 13.3 %collective-permute-start.31 = (f32[1,1,4,4,4,128]{5,4,3,2,1,0:T(4,128)S(1)}, f32[1,1,4,4,4,128]{5,4,3,2,1,0:T(4,128)S(1)}, u32[]{:S(2)}, u32[]{:S(2)}) collective-permute-start(f32[1,1,4,4,4,128]{5,4,3,2,1,0:T(4,128)S(1)} %bitcast.456), channel_id=1, source_target_pairs={{1,0},{2,1},{3,2},{4,3},{5,4},{6,5},{7,6},{8,7},{9,8},{10,9},{11,1... | collective-permute-start | bytes 98312 | tf_op jit(solution)/shard_map/ppermute | solution.py:32
  419.3 7.9 %collective-permute-start.30 = (f32[1,1,4,4,4,128]{5,4,3,2,1,0:T(4,128)S(1)}, f32[1,1,4,4,4,128]{5,4,3,2,1,0:T(4,128)S(1)}, u32[]{:S(2)}, u32[]{:S(2)}) collective-permute-start(f32[1,1,4,4,4,128]{5,4,3,2,1,0:T(4,128)S(1)} %bitcast.457), channel_id=1, source_target_pairs={{0,1},{1,2},{2,3},{3,4},{4,5},{5,6},{6,7},{7,8},{8,9},{9,10},{10,1... | collective-permute-start | bytes 98312 | tf_op jit(solution)/shard_map/ppermute | solution.py:31
  421.2 3.1 collective-permute-start.29
Sparse Core Ops, SparseCore 0:
  119.2 44.6 all-reduce.4
  166.5 29.1 all-reduce.6
  198.0 46.6 all-reduce.8
  246.9 74.1 all-reduce.10
